TPU v7x, 32 devices: a whole 2x2x4 slice. The times are simulated.
32 devices in a mesh: expert: 8 (over z, y), tensor: 4 (over x, core).
Axes of the slice: x: 2, y: 2, z: 4, core: 2. Of those that a mesh axis runs over, the one named last changes fastest.
Arguments:
- tokens: bfloat16 [1024, 2048], P('expert', 'tensor'), may hold values from -6 to 6
- grad_out: bfloat16 [1024, 2048], P('expert', 'tensor'), may hold values from -6 to 6
- route_weights: float32 [1024, 8], P('expert'), may hold values from 0.02 to 0.5
- expert_ids: int32 [1024, 8], P('expert'), may hold values from 0 to 15, all different within a row; in each aligned block of 128 rows (0 to 127, 128 to 255, ...) at most 96 rows name the same one
- gate_weight: bfloat16 [16, 2048, 768], P('expert', None, 'tensor'), may hold values from -0.125 to 0.125
- up_weight: bfloat16 [16, 2048, 768], P('expert', None, 'tensor'), may hold values from -0.125 to 0.125
- down_weight: bfloat16 [16, 768, 2048], P('expert', 'tensor'), may hold values from -0.21875 to 0.21875
- gate_adapter_first: bfloat16 [16, 2048, 64], P('expert'), may hold values from -0.125 to 0.125
- gate_adapter_second: bfloat16 [16, 64, 768], P('expert', None, 'tensor'), may hold values from -0.75 to 0.75
- up_adapter_first: bfloat16 [16, 2048, 64], P('expert'), may hold values from -0.125 to 0.125
- up_adapter_second: bfloat16 [16, 64, 768], P('expert', None, 'tensor'), may hold values from -0.75 to 0.75
- down_adapter_first: bfloat16 [16, 768, 64], P('expert', 'tensor'), may hold values from -0.21875 to 0.21875
- down_adapter_second: bfloat16 [16, 64, 2048], P('expert'), may hold values from -0.75 to 0.75
Outputs:
- grad_tokens: bfloat16 [1024, 2048], P('expert', 'tensor')
- gate_first_gradient: float32 [16, 2048, 64], P('expert', 'tensor')
- gate_second_gradient: float32 [16, 64, 768], P('expert', None, 'tensor')
- up_first_gradient: float32 [16, 2048, 64], P('expert', 'tensor')
- up_second_gradient: float32 [16, 64, 768], P('expert', None, 'tensor')
- down_first_gradient: float32 [16, 768, 64], P('expert', 'tensor')
- down_second_gradient: float32 [16, 64, 2048], P('expert', None, 'tensor')
Inputs may be any that keep to these rules, and one draw needn't show every extreme that they name: `expert_ids`: each token names 8 different experts. Among the 128 rows of one device no expert is named more than 96 times, a bound that some block reaches.
All inputs are finite; a program needn't handle non-finite values.
Results may differ from a plain program's by a relative error of at most 0.012.
Values may be sent and summed in bfloat16 or wider, within the bound.
A program may use at most 128 MiB of HBM per device.

v0:
```python
import jax
import jax.numpy as jnp
from jax import lax
from jax.sharding import PartitionSpec as P

adapter_scale = 0.5


def slot_positions(expert_ids, experts_all, capacity):
    tok_rows = expert_ids.shape[0]
    numbers = lax.broadcasted_iota(jnp.int32, (1, 1, experts_all), 2)
    picked = jnp.sum((expert_ids[:, :, None] == numbers).astype(jnp.float32), axis=1).astype(
        jnp.bfloat16
    )
    row_index = lax.broadcasted_iota(jnp.int32, (tok_rows, tok_rows), 0)
    col_index = lax.broadcasted_iota(jnp.int32, (tok_rows, tok_rows), 1)
    earlier = (row_index > col_index).astype(jnp.bfloat16)
    before = jnp.dot(earlier, picked, preferred_element_type=jnp.float32)
    slot_index = jnp.take_along_axis(before, expert_ids, axis=1).astype(jnp.int32)
    return expert_ids * capacity + slot_index


def fill_slots(values, positions, slot_count):
    width = values.shape[-1]
    flat = values.reshape(-1, width)
    return jnp.zeros((slot_count, width), values.dtype).at[positions.reshape(-1)].set(flat)


def local(
    tokens,
    grad_out,
    route_weights,
    expert_ids,
    gate_weight,
    up_weight,
    down_weight,
    gate_adapter_first,
    gate_adapter_second,
    up_adapter_first,
    up_adapter_second,
    down_adapter_first,
    down_adapter_second,
):
    single_float = jnp.float32
    brain_float_half = jnp.bfloat16
    tok_rows, top_count = expert_ids.shape
    local_experts = gate_weight.shape[0]
    sources = lax.axis_size("expert")
    experts_all = local_experts * sources
    capacity = 3 * tok_rows * top_count // (2 * experts_all)
    slot_count = experts_all * capacity
    positions = slot_positions(expert_ids, experts_all, capacity)
    width = tokens.shape[1]
    spread_in = jnp.broadcast_to(tokens[:, None, :], (tok_rows, top_count, width))
    scaled = (route_weights[:, :, None] * grad_out[:, None, :].astype(single_float)).astype(
        brain_float_half
    )
    send_in = fill_slots(spread_in, positions, slot_count)
    send_grad = fill_slots(scaled, positions, slot_count)
    part_in, part_grad = (
        lax.all_to_all(send_in, "expert", split_axis=0, concat_axis=0, tiled=True),
        lax.all_to_all(send_grad, "expert", split_axis=0, concat_axis=0, tiled=True),
    )
    recv_in, recv_grad = (
        lax.all_gather(part_in, "tensor", axis=1, tiled=True),
        lax.all_gather(part_grad, "tensor", axis=1, tiled=True),
    )
    hidden_width = recv_in.shape[1]
    routed_input = recv_in.reshape(sources, local_experts, capacity, hidden_width)
    routed_gradient = recv_grad.reshape(sources, local_experts, capacity, hidden_width)
    slice_width = hidden_width // lax.axis_size("tensor")
    slice_start = lax.axis_index("tensor") * slice_width
    adapter_gate_term = jnp.einsum(
        "mbtk,bkz->mbtz", routed_input, gate_adapter_first, preferred_element_type=single_float
    ).astype(brain_float_half)
    adapter_up_term = jnp.einsum(
        "mbtk,bkz->mbtz", routed_input, up_adapter_first, preferred_element_type=single_float
    ).astype(brain_float_half)
    gate_activation = jnp.einsum(
        "secd,edf->secf", routed_input, gate_weight, preferred_element_type=single_float
    )
    gate_activation = gate_activation + adapter_scale * jnp.einsum(
        "imal,mlt->imat",
        adapter_gate_term,
        gate_adapter_second,
        preferred_element_type=single_float,
    )
    up_activation = jnp.einsum(
        "secd,edf->secf", routed_input, up_weight, preferred_element_type=single_float
    )
    up_activation = up_activation + adapter_scale * jnp.einsum(
        "imal,mlt->imat", adapter_up_term, up_adapter_second, preferred_element_type=single_float
    )
    sigma = jax.nn.sigmoid(gate_activation)
    active = gate_activation * sigma
    hidden_activation = (active * up_activation).astype(brain_float_half)
    down_part = jnp.einsum(
        "secf,efr->secr", hidden_activation, down_adapter_first, preferred_element_type=single_float
    )
    down_total = lax.psum(down_part.astype(jnp.bfloat16), "tensor").astype(jnp.float32)
    backward_adapter_term = jnp.einsum(
        "secd,erd->secr", routed_gradient, down_adapter_second, preferred_element_type=single_float
    ).astype(brain_float_half)
    hidden_gradient = jnp.einsum(
        "secd,efd->secf", routed_gradient, down_weight, preferred_element_type=single_float
    )
    hidden_gradient = hidden_gradient + adapter_scale * jnp.einsum(
        "oamh,ath->oamt",
        backward_adapter_term,
        down_adapter_first,
        preferred_element_type=single_float,
    )
    gate_gradient = (
        hidden_gradient * up_activation * sigma * (1.0 + gate_activation * (1.0 - sigma))
    ).astype(brain_float_half)
    upward_gradient = (hidden_gradient * active).astype(brain_float_half)
    gate_part = jnp.einsum(
        "secf,erf->secr", gate_gradient, gate_adapter_second, preferred_element_type=single_float
    )
    up_part = jnp.einsum(
        "secf,erf->secr", upward_gradient, up_adapter_second, preferred_element_type=single_float
    )
    joined_weight = jnp.concatenate(
        (gate_weight, up_weight, gate_adapter_first, up_adapter_first), axis=2
    )
    joined_grad = jnp.concatenate(
        (
            gate_gradient,
            upward_gradient,
            gate_part.astype(brain_float_half) * adapter_scale,
            up_part.astype(brain_float_half) * adapter_scale,
        ),
        axis=3,
    )
    input_portion = (
        jnp.einsum(
            "secf,edf->secd", joined_grad, joined_weight, preferred_element_type=single_float
        )
        .astype(brain_float_half)
        .reshape(slot_count, hidden_width)
    )
    gate_total, up_total = (
        lax.psum(gate_part.astype(jnp.bfloat16), "tensor").astype(jnp.float32),
        lax.psum(up_part.astype(jnp.bfloat16), "tensor").astype(jnp.float32),
    )
    in_slice = lax.dynamic_slice_in_dim(routed_input, slice_start, slice_width, 3)
    grad_slice = lax.dynamic_slice_in_dim(routed_gradient, slice_start, slice_width, 3)
    gate_first_gradient = adapter_scale * jnp.einsum(
        "secd,secr->edr",
        in_slice,
        gate_total.astype(brain_float_half),
        preferred_element_type=single_float,
    )
    up_first_gradient = adapter_scale * jnp.einsum(
        "secd,secr->edr",
        in_slice,
        up_total.astype(brain_float_half),
        preferred_element_type=single_float,
    )
    gate_second_gradient = adapter_scale * jnp.einsum(
        "zdbq,zdbx->dqx", adapter_gate_term, gate_gradient, preferred_element_type=single_float
    )
    up_second_gradient = adapter_scale * jnp.einsum(
        "zdbq,zdbx->dqx", adapter_up_term, upward_gradient, preferred_element_type=single_float
    )
    down_first_gradient = adapter_scale * jnp.einsum(
        "qoax,qoap->oxp",
        hidden_activation,
        backward_adapter_term,
        preferred_element_type=single_float,
    )
    down_second_gradient = adapter_scale * jnp.einsum(
        "secr,secd->erd",
        down_total.astype(brain_float_half),
        grad_slice,
        preferred_element_type=single_float,
    )
    reduced = lax.psum_scatter(
        input_portion.astype(single_float).astype(jnp.bfloat16),
        "tensor",
        scatter_dimension=1,
        tiled=True,
    ).astype(jnp.float32)
    returned = lax.all_to_all(
        reduced.astype(jnp.bfloat16), "expert", split_axis=0, concat_axis=0, tiled=True
    ).astype(reduced.dtype)
    grad_tokens = jnp.sum(returned[positions], axis=1).astype(brain_float_half)
    return (
        grad_tokens,
        gate_first_gradient,
        gate_second_gradient,
        up_first_gradient,
        up_second_gradient,
        down_first_gradient,
        down_second_gradient,
    )


def solution(mesh):
    return jax.shard_map(
        local,
        mesh=mesh,
        in_specs=(
            P("expert", "tensor"),
            P("expert", "tensor"),
            P("expert", None),
            P("expert", None),
            P("expert", None, "tensor"),
            P("expert", None, "tensor"),
            P("expert", "tensor", None),
            P("expert", None, None),
            P("expert", None, "tensor"),
            P("expert", None, None),
            P("expert", None, "tensor"),
            P("expert", "tensor", None),
            P("expert", None, None),
        ),
        out_specs=(
            P("expert", "tensor"),
            P("expert", "tensor", None),
            P("expert", None, "tensor"),
            P("expert", "tensor", None),
            P("expert", None, "tensor"),
            P("expert", "tensor", None),
            P("expert", None, "tensor"),
        ),
        check_vma=False,
    )
```

profile of v0, /device:TPU:0, one launch (start us, length us, event | category | flops | bytes accessed | tf_op | source)
XLA Modules:
  0.0 321.8 jit_solution(6364558677875069623)
XLA Ops:
  7.2 0.8 bitcast_or_fusion
  8.0 0.7 convert_reduce_fusion
  8.7 0.1 copy.84
  8.9 0.1 fusion.80
  9.1 7.0 %gather_fusion.1 = f32[1024]{0:T(1024)S(1)} fusion(f32[128,16]{0,1:T(8,128)S(1)} %fusion.80, s32[1024]{0:T(1024)S(1)} %reshape.99), kind=kCustom, calls=%fused_computation.1 | custom fusion | bytes 16384 | tf_op jit(solution)/shard_map/jit(take_along_axis)/gather | solution.py:19
  16.3 0.1 copy.86
  16.5 5.6 %scatter_custom_fusion.1 = bf16[1536,512]{1,0:T(8,128)(2,1)S(1)} fusion(s32[1024]{0:T(1024)S(1)} %bitcast.192, bf16[]{:T(256)} %constant.14.clone.1, bf16[128,512]{1,0:T(8,128)(2,1)S(1)} %copy-done.15), kind=kCustom, calls=%fused_computation.78 | custom fusion | bytes 1703938 | tf_op jit(solution)/shard_map/scatter | solution.py:26
  22.1 44.3 %all_to_all.33 = bf16[8,192,512]{2,1,0:T(8,128)(2,1)} all-to-all(bf16[8,192,512]{2,1,0:T(8,128)(2,1)S(1)} %bitcast.190), channel_id=1, replica_groups=mesh['expert'=8,'tensor'=4] {'expert'}, dimensions={0} | all-to-all | bytes 3145728 | tf_op jit(solution)/shard_map/all_to_all | solution.py:61
  66.6 0.1 copy.87
  66.8 6.0 %scatter_custom_fusion = bf16[1536,512]{1,0:T(8,128)(2,1)S(1)} fusion(s32[1024]{0:T(1024)S(1)} %bitcast.193, f32[128,512]{1,0:T(8,128)S(1)} %convert_element_type.93, f32[1024]{0:T(1024)S(1)} %mul.92, bf16[]{:T(256)} %constant.14.clone.1), kind=kCustom, calls=%fused_computation.77 | custom fusion | flops 1048576 | bytes 1839106 | tf_op jit(solution)/shard_map/scatter | solution.py:26
  72.7 40.2 %all_to_all.34 = bf16[8,192,512]{2,1,0:T(8,128)(2,1)} all-to-all(bf16[8,192,512]{2,1,0:T(8,128)(2,1)S(1)} %bitcast.189), channel_id=1, replica_groups=mesh['expert'=8,'tensor'=4] {'expert'}, dimensions={0} | all-to-all | bytes 3145728 | tf_op jit(solution)/shard_map/all_to_all | solution.py:62
  113.0 1.3 copy-done.3
  114.3 2.5 copy.80
  116.8 3.7 %copy.81 = bf16[2,2048,192]{2,1,0:T(8,128)(2,1)} copy(bf16[2,2048,192]{1,2,0:T(8,128)(2,1)} %param.18) | data formatting | bytes 3145728 | tf_op args[5]
  120.5 2.5 copy.82
  123.0 2.5 copy.83
  125.5 5.4 %fusion.37 = bf16[8,2,96,64]{2,3,0,1:T(8,128)(2,1)S(1)} fusion(bf16[2,2048,64]{1,2,0:T(8,128)(2,1)} %param.20, bf16[8,2,96,2048]{3,2,1,0:T(8,128)(2,1)} %bitcast.194), kind=kOutput, calls=%fused_computation.61 | convolution fusion | flops 402751488 | bytes 7012352 | tf_op jit(solution)/shard_map/mbtk,bkz->mbtz/dot_general | solution.py:73
  130.9 3.1 fusion.36
  134.0 3.1 fusion.14
  137.1 3.0 fusion.16
  140.1 19.9 %all-gather.3.cloned.1.call-done = bf16[1536,2048]{1,0:T(8,128)(2,1)} async-done(((bf16[1536,512]{1,0:T(8,128)(2,1)}), bf16[1536,2048]{1,0:T(8,128)(2,1)}) %all-gather.3.cloned.1.call-update) | async-done | bytes 6291472 | tf_op jit(solution)/shard_map/all_gather | solution.py:66
  159.9 5.3 %fusion.35 = bf16[8,2,96,64]{2,3,0,1:T(8,128)(2,1)S(1)} fusion(bf16[2,64,2048]{2,1,0:T(8,128)(2,1)S(1)} %copy-done.22, bf16[8,2,96,2048]{3,2,1,0:T(8,128)(2,1)} %bitcast.200), kind=kOutput, calls=%fused_computation.59 | convolution fusion | flops 402751488 | bytes 7012352 | tf_op jit(solution)/shard_map/secd,erd->secr/dot_general | solution.py:101
  165.3 1.8 fusion.18
  167.2 0.4 multiply_add_fusion
  167.6 0.4 copy-done.12
  168.0 0.4 multiply_add_fusion.2
  168.4 0.5 copy-done.13
  169.0 0.6 copy-done.25
  169.6 1.3 fusion.27
  170.9 1.2 broadcast_multiply_fusion
  172.1 1.2 broadcast_multiply_fusion.1
  173.3 1.9 copy.94
  175.2 1.9 copy.95
  177.1 8.9 %convert_bitcast_fusion = bf16[8,2,96,2048]{3,2,0,1:T(8,128)(2,1)} fusion(bf16[2,2048,64]{2,1,0:T(8,128)(2,1)} %copy.83, bf16[2,2048,64]{2,1,0:T(8,128)(2,1)S(1)} %copy-done.6, bf16[2,2048,192]{2,1,0:T(8,128)(2,1)} %copy.81, bf16[2,2048,192]{2,1,0:T(8,128)(2,1)} %copy.80, bf16[8,2,96,64]{3,2,0,1:T(8,128)(2,1)} %copy.95, bf16[8,2,96,64]{3,2,0,1:T(8,128)(2,1)} %copy.94, ...), kind=kOutput, calls=%fused_computation.4 | convolution fusion | flops 3247439872 | bytes 12058624 | tf_op jit(solution)/shard_map/secf,edf->secd/dot_general | solution.py:136
  186.0 6.6 %copy.96 = bf16[8,2,96,2048]{3,2,1,0:T(8,128)(2,1)} copy(bf16[8,2,96,2048]{3,2,0,1:T(8,128)(2,1)} %convert_bitcast_fusion) | data formatting | bytes 12582912 | tf_op jit(solution)/shard_map/convert_element_type | solution.py:139
  192.6 58.0 %reduce-scatter.2.cloned.1.call-done = bf16[1536,512]{1,0:T(8,128)(2,1)} async-done(((bf16[1536,2048]{1,0:T(8,128)(2,1)}), bf16[1536,512]{1,0:T(8,128)(2,1)}) %reduce-scatter.2.cloned.1.call-update) | async-done | bytes 1572880 | tf_op jit(solution)/shard_map/reduce_scatter | solution.py:178
  250.6 5.6 %all-to-all-start.2 = ((bf16[8,192,512]{2,1,0:T(8,128)(2,1)}), bf16[8,192,512]{2,1,0:T(8,128)(2,1)S(1)}, u32[]{:S(2)}, u32[]{:S(2)}) async-start(bf16[8,192,512]{2,1,0:T(8,128)(2,1)} %bitcast.191), calls=%async_computation.3 | async-start | bytes 3145728 | tf_op jit(solution)/shard_map/all_to_all | solution.py:184
  256.5 1.1 fusion.40
  257.7 2.1 fusion.59
  259.8 1.9 fusion.60
  261.7 1.0 fusion.61
  262.7 32.6 %all-reduce.3.cloned.1.call-done = (bf16[8,2,96,64]{2,3,0,1:T(8,128)(2,1)}, bf16[8,2,96,64]{2,3,0,1:T(8,128)(2,1)}, bf16[8,2,96,64]{2,3,0,1:T(8,128)(2,1)}) async-done(((bf16[8,2,96,64]{2,3,0,1:T(8,128)(2,1)}, bf16[8,2,96,64]{2,3,0,1:T(8,128)(2,1)}, bf16[8,2,96,64]{2,3,0,1:T(8,128)(2,1)}), (bf16[8,2,96,64]{2,3,0,1:T(8,128)(2,1)}, bf16[8,2,96,64]{2,3,0,1:T(8,128)(2,1)}, ...) | async-done | bytes 589840 | tf_op jit(solution)/shard_map/psum | solution.py:143
  295.2 2.7 fusion.50
  297.9 2.6 fusion.56
  300.5 2.5 fusion.53
  303.0 2.2 bitcast_convert_fusion
  305.2 7.3 %gather_fusion = f32[1024,512]{1,0:T(8,128)} fusion(f32[1536,512]{1,0:T(8,128)} %bitcast_convert_fusion, s32[1024]{0:T(1024)S(1)} %broadcast_clamp_fusion), kind=kCustom, calls=%fused_computation | custom fusion | bytes 4198400 | tf_op jit(solution)/shard_map/gather | solution.py:187
  312.5 2.8 bitcast_reduce_fusion
  (69 shorter events, 1.0 us)
Async XLA Ops:
  7.2 158.1 %copy-start = (bf16[2,192,2048]{2,1,0:T(8,128)(2,1)S(1)}, bf16[2,192,2048]{2,1,0:T(8,128)(2,1)}, u32[]{:S(2)}) copy-start(bf16[2,192,2048]{2,1,0:T(8,128)(2,1)} %param.19) | copy-start | bytes 4718596
  7.2 118.3 %all-gather.5.cloned.1.call-start = ((), (), s32[]{:S(2)}) async-start(), calls=%async_computation.5 | async-start | bytes 7864320 | tf_op jit(solution)/shard_map/all_gather | solution.py:65
  9.1 7.2 %copy-start.18 = (s32[128,8]{0,1:T(8,128)S(1)}, s32[128,8]{0,1:T(8,128)}, u32[]{:S(2)}) copy-start(s32[128,8]{0,1:T(8,128)} %param.16) | copy-start | bytes 12292
  9.1 7.4 %copy-start.15 = (bf16[128,512]{1,0:T(8,128)(2,1)S(1)}, bf16[128,512]{1,0:T(8,128)(2,1)}, u32[]{:S(2)}) copy-start(bf16[128,512]{1,0:T(8,128)(2,1)} %param.13) | copy-start | bytes 393220
  22.1 44.4 %copy-start.16 = (bf16[128,512]{1,0:T(8,128)(2,1)S(1)}, bf16[128,512]{1,0:T(8,128)(2,1)}, u32[]{:S(2)}) copy-start(bf16[128,512]{1,0:T(8,128)(2,1)} %param.14) | copy-start | bytes 393220
  22.1 44.5 %copy-start.19 = (f32[128,8]{0,1:T(8,128)S(1)}, f32[128,8]{0,1:T(8,128)}, u32[]{:S(2)}) copy-start(f32[128,8]{0,1:T(8,128)} %param.15) | copy-start | bytes 12292
  66.5 93.5 %all-gather.3.cloned.1.call-start = ((), (), s32[]{:S(2)}) async-start(), calls=%async_computation.4 | async-start | bytes 7864320 | tf_op jit(solution)/shard_map/all_gather | solution.py:66
  112.9 1.4 copy-start.3
  113.0 137.7 %reduce-scatter.2.cloned.1.call-start = ((), (), s32[]{:S(2)}) async-start(), calls=%async_computation.6 | async-start | bytes 7864320 | tf_op jit(solution)/shard_map/reduce_scatter | solution.py:178
  125.5 5.4 %copy-start.11 = (bf16[2,2048,64]{1,2,0:T(8,128)(2,1)S(1)}, bf16[2,2048,64]{1,2,0:T(8,128)(2,1)}, u32[]{:S(2)}) copy-start(bf16[2,2048,64]{1,2,0:T(8,128)(2,1)} %param.22) | copy-start | bytes 1572868
  125.5 5.4 %copy-start.20 = (bf16[1536,2048]{1,0:T(8,128)(2,1)S(1)}, bf16[1536,2048]{1,0:T(8,128)(2,1)}, u32[]{:S(2)}) copy-start(bf16[1536,2048]{1,0:T(8,128)(2,1)} %all-gather.5.cloned.1.call-done) | copy-start | bytes 18874372
  130.9 36.2 %copy-start.7 = (bf16[8,2,96,64]{2,3,0,1:T(8,128)(2,1)}, bf16[8,2,96,64]{2,3,0,1:T(8,128)(2,1)S(1)}, u32[]{:S(2)}) copy-start(bf16[8,2,96,64]{2,3,0,1:T(8,128)(2,1)S(1)} %fusion.37) | copy-start | bytes 589828
  134.0 3.1 copy-start.4
  137.1 22.8 %copy-start.22 = (bf16[2,64,2048]{2,1,0:T(8,128)(2,1)S(1)}, bf16[2,64,2048]{2,1,0:T(8,128)(2,1)}, u32[]{:S(2)}) copy-start(bf16[2,64,2048]{2,1,0:T(8,128)(2,1)} %param.25) | copy-start | bytes 1572868
  159.9 5.3 %copy-start.21 = (bf16[1536,2048]{1,0:T(8,128)(2,1)S(1)}, bf16[1536,2048]{1,0:T(8,128)(2,1)}, u32[]{:S(2)}) copy-start(bf16[1536,2048]{1,0:T(8,128)(2,1)} %all-gather.3.cloned.1.call-done) | copy-start | bytes 18874372
  165.3 2.3 copy-start.9
  165.3 1.9 copy-start.5
  165.3 1.9 copy-start.14
  167.2 0.8 copy-start.12
  168.0 0.9 copy-start.13
  168.0 1.0 copy-start.17
  168.0 1.5 copy-start.25
  170.9 15.2 %copy-start.2 = (bf16[8,2,96,192]{3,2,0,1:T(8,128)(2,1)}, bf16[8,2,96,192]{3,2,0,1:T(8,128)(2,1)S(1)}, u32[]{:S(2)}) copy-start(bf16[8,2,96,192]{3,2,0,1:T(8,128)(2,1)S(1)} %get-tuple-element.13) | copy-start | bytes 1769476
  170.9 6.2 %copy-start.6 = (bf16[2,2048,64]{2,1,0:T(8,128)(2,1)S(1)}, bf16[2,2048,64]{2,1,0:T(8,128)(2,1)}, u32[]{:S(2)}) copy-start(bf16[2,2048,64]{2,1,0:T(8,128)(2,1)} %copy.82) | copy-start | bytes 1572868
  250.6 7.0 %copy-start.8 = (bf16[8,2,96,64]{2,3,0,1:T(8,128)(2,1)S(1)}, bf16[8,2,96,64]{2,3,0,1:T(8,128)(2,1)}, u32[]{:S(2)}) copy-start(bf16[8,2,96,64]{2,3,0,1:T(8,128)(2,1)} %copy-done.7) | copy-start | bytes 589828
  250.6 52.4 %all-to-all-start.2 = ((bf16[8,192,512]{2,1,0:T(8,128)(2,1)}), bf16[8,192,512]{2,1,0:T(8,128)(2,1)S(1)}, u32[]{:S(2)}, u32[]{:S(2)}) async-start(bf16[8,192,512]{2,1,0:T(8,128)(2,1)} %bitcast.191), calls=%async_computation.3 | async-start | bytes 3145728 | tf_op jit(solution)/shard_map/all_to_all | solution.py:184
  256.3 39.0 %all-reduce.3.cloned.1.call-start = ((), (), s32[]{:S(2)}) async-start(), calls=%async_computation.7 | async-start | bytes 1572864 | tf_op jit(solution)/shard_map/psum | solution.py:143
  257.7 4.0 %copy-start.10 = (bf16[8,2,96,64]{2,3,0,1:T(8,128)(2,1)S(1)}, bf16[8,2,96,64]{2,3,0,1:T(8,128)(2,1)}, u32[]{:S(2)}) copy-start(bf16[8,2,96,64]{2,3,0,1:T(8,128)(2,1)} %copy-done.9) | copy-start | bytes 589828
  295.2 2.7 copy-start.24
  297.9 2.6 copy-start.23
  305.2 10.1 %copy-start.1 = (bf16[2,192,2048]{2,1,0:T(8,128)(2,1)S(1)}, bf16[2,192,2048]{2,1,0:T(8,128)(2,1)}, u32[]{:S(2)}) copy-start(bf16[2,192,2048]{2,1,0:T(8,128)(2,1)} %param.19) | copy-start | bytes 4718596
Sparse Core Ops, SparseCore 0:
  66.6 45.3 all-gather.4
  113.6 46.3 all-gather.2
  192.7 57.8 reduce-scatter.1
  259.9 35.3 all-reduce.2
where the time goes:
time: 323 us; the launch traced here: 322 us
  waiting for transfers between devices  110 us (34%)
  blocking collectives  84.5 us (26%)
  matrix products  49.2 us (15%)
  local copies, waits for them, and re-layouts  45.3 us (14%)
  between operations  14.1 us (4%)
  other arithmetic  12.5 us (4%)
  starting transfers between devices  5.81 us (2%)
    reduce_scatter x1, waiting for transfers between devices, local(): lax.psum_scatter(input_portion.astype(single_float).astype(jnp.bfloat16),...  58 us
    all_to_all x1, blocking collectives, local(): lax.all_to_all(send_in, 'expert', split_axis=0, concat_axis=0, tiled=True)  44.3 us
    all_to_all x1, blocking collectives, local(): lax.all_to_all(send_grad, 'expert', split_axis=0, concat_axis=0, tiled=True)  40.2 us
    psum x1, waiting for transfers between devices, local(): lax.psum(gate_part.astype(jnp.bfloat16), 'tensor').astype(jnp.float32)  32.6 us
    all_gather x1, waiting for transfers between devices, local(): lax.all_gather(part_grad, 'tensor', axis=1, tiled=True)  19.9 us
    unnamed x57, local copies, waits for them, and re-layouts  14.2 us
    dot_general x1, matrix products, local(): jnp.einsum('secf,edf->secd', joined_grad, joined_weight, preferred_elemen...  8.95 us
    gather x5, local copies, waits for them, and re-layouts, slot_positions(): jnp.take_along_axis(before, expert_ids, axis=1).astype(jnp.int32)  7.36 us
  transfers between devices with their start and end apart: 5, of which 3 were waited for; matrix products, arithmetic and copies ran while one was open for 14% of the time, Pallas kernels for 0%

commit v1 on v0

--- a/solution.py
+++ b/solution.py
@@ -63,7 +63,7 @@
     )
     recv_in, recv_grad = (
         lax.all_gather(part_in, "tensor", axis=1, tiled=True),
-        lax.all_gather(part_grad, "tensor", axis=1, tiled=True),
+        jnp.concatenate(lax.all_gather(part_grad, "tensor"), axis=1),
     )
     hidden_width = recv_in.shape[1]
     routed_input = recv_in.reshape(sources, local_experts, capacity, hidden_width)

time: 323 us -> 342 us (1.059)
  local copies, waits for them, and re-layouts: 45.3 us -> 64 us
    another operation x0 -> x1, local copies, waits for them, and re-layouts: none -> 11.2 us  [local(): recv_grad.reshape(sources, local_experts, capacity, hidden_width)]
    reshape x0 -> x1, local copies, waits for them, and re-layouts: none -> 10.4 us  [local(): jnp.concatenate(lax.all_gather(part_grad, 'tensor'), axis=1)]
    unnamed x57 -> x51, local copies, waits for them, and re-layouts: 14.2 us -> 14 us
where the time goes in v1:
time: 342 us; the launch traced here: 341 us
  waiting for transfers between devices  111 us (32%)
  blocking collectives  84.5 us (25%)
  local copies, waits for them, and re-layouts  64 us (19%)
  matrix products  49.1 us (14%)
  between operations  14 us (4%)
  other arithmetic  12.5 us (4%)
  starting transfers between devices  5.85 us (2%)
    reduce_scatter x1, waiting for transfers between devices, local(): lax.psum_scatter(input_portion.astype(single_float).astype(jnp.bfloat16),...  58 us
    all_to_all x1, blocking collectives, local(): lax.all_to_all(send_in, 'expert', split_axis=0, concat_axis=0, tiled=True)  44.3 us
    all_to_all x1, blocking collectives, local(): lax.all_to_all(send_grad, 'expert', split_axis=0, concat_axis=0, tiled=True)  40.2 us
    psum x1, waiting for transfers between devices, local(): lax.psum(gate_part.astype(jnp.bfloat16), 'tensor').astype(jnp.float32)  32.6 us
    all_gather x1, waiting for transfers between devices, local(): lax.all_gather(part_grad, 'tensor')  19.9 us
    unnamed x51, local copies, waits for them, and re-layouts  14 us
    another operation x1, local copies, waits for them, and re-layouts, local(): recv_grad.reshape(sources, local_experts, capacity, hidden_width)  11.2 us
    reshape x1, local copies, waits for them, and re-layouts, local(): jnp.concatenate(lax.all_gather(part_grad, 'tensor'), axis=1)  10.4 us
  transfers between devices with their start and end apart: 5, of which 3 were waited for; matrix products, arithmetic and copies ran while one was open for 14% of the time, Pallas kernels for 0%

profile of v1, /device:TPU:0, one launch (start us, length us, event | category | flops | bytes accessed | tf_op | source)
XLA Modules:
  0.0 340.6 jit_solution(9019091004739077311)
XLA Ops:
  7.2 0.8 bitcast_or_fusion
  8.0 0.7 convert_reduce_fusion
  8.9 0.1 fusion.80
  9.1 7.0 %gather_fusion.1 = f32[1024]{0:T(1024)S(1)} fusion(f32[128,16]{0,1:T(8,128)S(1)} %fusion.80, s32[1024]{0:T(1024)S(1)} %reshape.100), kind=kCustom, calls=%fused_computation.1 | custom fusion | bytes 16384 | tf_op jit(solution)/shard_map/jit(take_along_axis)/gather | solution.py:19
  16.5 5.6 %scatter_custom_fusion.1 = bf16[1536,512]{1,0:T(8,128)(2,1)S(1)} fusion(s32[1024]{0:T(1024)S(1)} %bitcast.193, bf16[]{:T(256)} %constant.14.clone.1, bf16[128,512]{1,0:T(8,128)(2,1)S(1)} %copy-done.13), kind=kCustom, calls=%fused_computation.78 | custom fusion | bytes 1703938 | tf_op jit(solution)/shard_map/scatter | solution.py:26
  22.1 44.3 %all_to_all.30 = bf16[8,192,512]{2,1,0:T(8,128)(2,1)} all-to-all(bf16[8,192,512]{2,1,0:T(8,128)(2,1)S(1)} %bitcast.191), channel_id=1, replica_groups=mesh['expert'=8,'tensor'=4] {'expert'}, dimensions={0} | all-to-all | bytes 3145728 | tf_op jit(solution)/shard_map/all_to_all | solution.py:61
  66.8 6.0 %scatter_custom_fusion = bf16[1536,512]{1,0:T(8,128)(2,1)S(1)} fusion(s32[1024]{0:T(1024)S(1)} %bitcast.194, f32[128,512]{1,0:T(8,128)S(1)} %convert_element_type.93, f32[1024]{0:T(1024)S(1)} %mul.92, bf16[]{:T(256)} %constant.14.clone.1), kind=kCustom, calls=%fused_computation.77 | custom fusion | flops 1048576 | bytes 1839106 | tf_op jit(solution)/shard_map/scatter | solution.py:26
  72.7 40.2 %all_to_all.31 = bf16[8,192,512]{2,1,0:T(8,128)(2,1)} all-to-all(bf16[8,192,512]{2,1,0:T(8,128)(2,1)S(1)} %bitcast.190), channel_id=1, replica_groups=mesh['expert'=8,'tensor'=4] {'expert'}, dimensions={0} | all-to-all | bytes 3145728 | tf_op jit(solution)/shard_map/all_to_all | solution.py:62
  113.0 0.2 reduce-scatter.2.cloned.1.call-start
  113.2 1.2 copy-done.4
  114.3 2.4 copy.135
  116.8 3.7 %copy.136 = bf16[2,2048,192]{2,1,0:T(8,128)(2,1)} copy(bf16[2,2048,192]{1,2,0:T(8,128)(2,1)} %param.18) | data formatting | bytes 3145728 | tf_op args[5]
  120.5 2.4 copy.137
  122.9 2.5 copy.138
  125.4 5.4 %fusion.37 = bf16[8,2,96,64]{2,3,0,1:T(8,128)(2,1)S(1)} fusion(bf16[2,2048,64]{1,2,0:T(8,128)(2,1)} %param.20, bf16[8,2,96,2048]{3,2,1,0:T(8,128)(2,1)} %bitcast.195), kind=kOutput, calls=%fused_computation.61 | convolution fusion | flops 402751488 | bytes 7012352 | tf_op jit(solution)/shard_map/mbtk,bkz->mbtz/dot_general | solution.py:73
  130.9 3.1 fusion.36
  134.0 3.1 fusion.14
  137.0 3.1 fusion.16
  140.1 19.9 %all-gather.3.cloned.1.call-done = bf16[4,1536,512]{2,1,0:T(8,128)(2,1)} async-done(((bf16[1,1536,512]{2,1,0:T(8,128)(2,1)}), bf16[4,1536,512]{2,1,0:T(8,128)(2,1)}) %all-gather.3.cloned.1.call-update) | async-done | bytes 6291472 | tf_op jit(solution)/shard_map/all_gather | solution.py:66
  159.9 10.4 %copy.143 = bf16[1536,4,512]{2,1,0:T(4,128)(2,1)} copy(bf16[1536,4,512]{2,0,1:T(8,128)(2,1)} %bitcast.187) | data formatting | bytes 12582912 | tf_op jit(solution)/shard_map/reshape | solution.py:66
  170.4 11.2 %reshape_reshape.3 = bf16[8,2,96,2048]{3,2,1,0:T(8,128)(2,1)} reshape(bf16[1536,4,512]{2,1,0:T(4,128)(2,1)} %copy.143) | data formatting | bytes 12582912 | tf_op jit(solution)/shard_map/reshape;reshape | solution.py:70
  181.5 5.3 %fusion.35 = bf16[8,2,96,64]{2,3,0,1:T(8,128)(2,1)S(1)} fusion(bf16[2,64,2048]{2,1,0:T(8,128)(2,1)S(1)} %copy-done.19, bf16[8,2,96,2048]{3,2,1,0:T(8,128)(2,1)} %reshape_reshape.3), kind=kOutput, calls=%fused_computation.59 | convolution fusion | flops 402751488 | bytes 7012352 | tf_op jit(solution)/shard_map/secd,erd->secr/dot_general | solution.py:101
  186.9 1.9 fusion.18
  188.9 0.4 multiply_add_fusion
  189.3 0.4 copy-done.10
  189.7 0.4 multiply_add_fusion.2
  190.1 0.5 copy-done.11
  190.7 0.6 copy-done.22
  191.2 1.1 fusion.27
  192.4 1.1 broadcast_multiply_fusion
  193.5 1.1 broadcast_multiply_fusion.1
  194.6 0.9 copy.150
  195.5 0.2 copy.151
  195.7 9.1 %convert_bitcast_fusion = bf16[8,2,96,2048]{3,2,0,1:T(8,128)(2,1)} fusion(bf16[2,2048,64]{2,1,0:T(8,128)(2,1)} %copy.138, bf16[2,2048,64]{2,1,0:T(8,128)(2,1)} %copy.137, bf16[2,2048,192]{2,1,0:T(8,128)(2,1)} %copy.136, bf16[2,2048,192]{2,1,0:T(8,128)(2,1)} %copy.135, bf16[8,2,96,64]{3,2,0,1:T(8,128)(2,1)S(1)} %copy.151, bf16[8,2,96,64]{3,2,0,1:T(8,128)(2,1)} %copy.150, ...), kind=kOutput, calls=%fused_computation.4 | convolution fusion | flops 3247439872 | bytes 12058624 | tf_op jit(solution)/shard_map/secf,edf->secd/dot_general | solution.py:136
  204.9 6.6 %copy.152 = bf16[8,2,96,2048]{3,2,1,0:T(8,128)(2,1)} copy(bf16[8,2,96,2048]{3,2,0,1:T(8,128)(2,1)} %convert_bitcast_fusion) | data formatting | bytes 12582912 | tf_op jit(solution)/shard_map/convert_element_type | solution.py:139
  211.5 58.0 %reduce-scatter.2.cloned.1.call-done = bf16[1536,512]{1,0:T(8,128)(2,1)} async-done(((bf16[1536,2048]{1,0:T(8,128)(2,1)}), bf16[1536,512]{1,0:T(8,128)(2,1)}) %reduce-scatter.2.cloned.1.call-update) | async-done | bytes 1572880 | tf_op jit(solution)/shard_map/reduce_scatter | solution.py:178
  269.5 5.5 %all-to-all-start.2 = ((bf16[8,192,512]{2,1,0:T(8,128)(2,1)}), bf16[8,192,512]{2,1,0:T(8,128)(2,1)S(1)}, u32[]{:S(2)}, u32[]{:S(2)}) async-start(bf16[8,192,512]{2,1,0:T(8,128)(2,1)} %bitcast.192), calls=%async_computation.3 | async-start | bytes 3145728 | tf_op jit(solution)/shard_map/all_to_all | solution.py:184
  275.2 1.1 fusion.40
  276.4 2.1 fusion.59
  278.5 1.9 fusion.60
  280.4 1.0 fusion.61
  281.4 32.6 %all-reduce.3.cloned.1.call-done = (bf16[8,2,96,64]{2,3,0,1:T(8,128)(2,1)}, bf16[8,2,96,64]{2,3,0,1:T(8,128)(2,1)}, bf16[8,2,96,64]{2,3,0,1:T(8,128)(2,1)}) async-done(((bf16[8,2,96,64]{2,3,0,1:T(8,128)(2,1)}, bf16[8,2,96,64]{2,3,0,1:T(8,128)(2,1)}, bf16[8,2,96,64]{2,3,0,1:T(8,128)(2,1)}), (bf16[8,2,96,64]{2,3,0,1:T(8,128)(2,1)}, bf16[8,2,96,64]{2,3,0,1:T(8,128)(2,1)}, ...) | async-done | bytes 589840 | tf_op jit(solution)/shard_map/psum | solution.py:143
  314.0 2.7 fusion.50
  316.7 2.6 fusion.56
  319.2 2.5 fusion.53
  321.8 2.2 bitcast_convert_fusion
  324.0 7.3 %gather_fusion = f32[1024,512]{1,0:T(8,128)} fusion(f32[1536,512]{1,0:T(8,128)} %bitcast_convert_fusion, s32[1024]{0:T(1024)S(1)} %broadcast_clamp_fusion), kind=kCustom, calls=%fused_computation | custom fusion | bytes 4198400 | tf_op jit(solution)/shard_map/gather | solution.py:187
  331.3 2.8 bitcast_reduce_fusion
  (65 shorter events, 1.3 us)
Async XLA Ops:
  7.2 179.7 %copy-start = (bf16[2,192,2048]{2,1,0:T(8,128)(2,1)S(1)}, bf16[2,192,2048]{2,1,0:T(8,128)(2,1)}, u32[]{:S(2)}) copy-start(bf16[2,192,2048]{2,1,0:T(8,128)(2,1)} %param.19) | copy-start | bytes 4718596
  7.2 118.3 %all-gather.5.cloned.1.call-start = ((), (), s32[]{:S(2)}) async-start(), calls=%async_computation.5 | async-start | bytes 7864320 | tf_op jit(solution)/shard_map/all_gather | solution.py:65
  9.1 7.2 %copy-start.16 = (s32[128,8]{0,1:T(8,128)S(1)}, s32[128,8]{0,1:T(8,128)}, u32[]{:S(2)}) copy-start(s32[128,8]{0,1:T(8,128)} %param.16) | copy-start | bytes 12292
  9.1 7.4 %copy-start.13 = (bf16[128,512]{1,0:T(8,128)(2,1)S(1)}, bf16[128,512]{1,0:T(8,128)(2,1)}, u32[]{:S(2)}) copy-start(bf16[128,512]{1,0:T(8,128)(2,1)} %param.13) | copy-start | bytes 393220
  22.1 44.4 %copy-start.14 = (bf16[128,512]{1,0:T(8,128)(2,1)S(1)}, bf16[128,512]{1,0:T(8,128)(2,1)}, u32[]{:S(2)}) copy-start(bf16[128,512]{1,0:T(8,128)(2,1)} %param.14) | copy-start | bytes 393220
  22.1 44.5 %copy-start.17 = (f32[128,8]{0,1:T(8,128)S(1)}, f32[128,8]{0,1:T(8,128)}, u32[]{:S(2)}) copy-start(f32[128,8]{0,1:T(8,128)} %param.15) | copy-start | bytes 12292
  66.5 93.5 %all-gather.3.cloned.1.call-start = ((), (), s32[]{:S(2)}) async-start(), calls=%async_computation.4 | async-start | bytes 7864320 | tf_op jit(solution)/shard_map/all_gather | solution.py:66
  112.9 1.4 copy-start.4
  113.0 156.5 %reduce-scatter.2.cloned.1.call-start = ((), (), s32[]{:S(2)}) async-start(), calls=%async_computation.6 | async-start | bytes 7864320 | tf_op jit(solution)/shard_map/reduce_scatter | solution.py:178
  125.4 5.4 %copy-start.9 = (bf16[2,2048,64]{1,2,0:T(8,128)(2,1)S(1)}, bf16[2,2048,64]{1,2,0:T(8,128)(2,1)}, u32[]{:S(2)}) copy-start(bf16[2,2048,64]{1,2,0:T(8,128)(2,1)} %param.22) | copy-start | bytes 1572868
  125.4 5.4 %copy-start.18 = (bf16[1536,2048]{1,0:T(8,128)(2,1)S(1)}, bf16[1536,2048]{1,0:T(8,128)(2,1)}, u32[]{:S(2)}) copy-start(bf16[1536,2048]{1,0:T(8,128)(2,1)} %all-gather.5.cloned.1.call-done) | copy-start | bytes 18874372
  134.0 3.1 copy-start.5
  170.4 11.2 %copy-start.19 = (bf16[2,64,2048]{2,1,0:T(8,128)(2,1)S(1)}, bf16[2,64,2048]{2,1,0:T(8,128)(2,1)}, u32[]{:S(2)}) copy-start(bf16[2,64,2048]{2,1,0:T(8,128)(2,1)} %param.25) | copy-start | bytes 1572868
  181.5 5.3 %copy-start.2 = (bf16[8,2,96,2048]{3,2,1,0:T(8,128)(2,1)S(1)}, bf16[8,2,96,2048]{3,2,1,0:T(8,128)(2,1)}, u32[]{:S(2)}) copy-start(bf16[8,2,96,2048]{3,2,1,0:T(8,128)(2,1)} %reshape_reshape.3) | copy-start | bytes 18874372
  186.9 2.4 copy-start.7
  186.9 1.9 copy-start.6
  186.9 1.9 copy-start.12
  188.9 0.8 copy-start.10
  189.7 0.9 copy-start.11
  189.7 1.0 copy-start.15
  189.7 1.5 copy-start.22
  192.3 12.5 %copy-start.3 = (bf16[8,2,96,192]{3,2,0,1:T(8,128)(2,1)}, bf16[8,2,96,192]{3,2,0,1:T(8,128)(2,1)S(1)}, u32[]{:S(2)}) copy-start(bf16[8,2,96,192]{3,2,0,1:T(8,128)(2,1)S(1)} %get-tuple-element.13) | copy-start | bytes 1769476
  269.5 52.3 %all-to-all-start.2 = ((bf16[8,192,512]{2,1,0:T(8,128)(2,1)}), bf16[8,192,512]{2,1,0:T(8,128)(2,1)S(1)}, u32[]{:S(2)}, u32[]{:S(2)}) async-start(bf16[8,192,512]{2,1,0:T(8,128)(2,1)} %bitcast.192), calls=%async_computation.3 | async-start | bytes 3145728 | tf_op jit(solution)/shard_map/all_to_all | solution.py:184
  275.0 39.0 %all-reduce.3.cloned.1.call-start = ((), (), s32[]{:S(2)}) async-start(), calls=%async_computation.7 | async-start | bytes 1572864 | tf_op jit(solution)/shard_map/psum | solution.py:143
  276.4 4.0 %copy-start.8 = (bf16[8,2,96,64]{2,3,0,1:T(8,128)(2,1)S(1)}, bf16[8,2,96,64]{2,3,0,1:T(8,128)(2,1)}, u32[]{:S(2)}) copy-start(bf16[8,2,96,64]{2,3,0,1:T(8,128)(2,1)} %copy-done.7) | copy-start | bytes 589828
  314.0 2.7 copy-start.21
  316.6 2.6 copy-start.20
  324.0 10.1 %copy-start.1 = (bf16[2,192,2048]{2,1,0:T(8,128)(2,1)S(1)}, bf16[2,192,2048]{2,1,0:T(8,128)(2,1)}, u32[]{:S(2)}) copy-start(bf16[2,192,2048]{2,1,0:T(8,128)(2,1)} %param.19) | copy-start | bytes 4718596
Sparse Core Ops, SparseCore 0:
  66.6 45.3 all-gather.4
  113.6 46.3 all-gather.2
  211.6 57.8 reduce-scatter.1
  278.6 35.3 all-reduce.2
